TPU v7x, 512 devices: a whole 4x8x8 slice. The times are simulated.
512 devices in a mesh: member: 16 (over x, y_hi, core), tile: 32 (over y_lo, z).
Axes of the slice: x: 4, y: 8 (y_hi: 2, y_lo: 4; y = y_hi * 4 + y_lo), z: 8, core: 2. Of those that a mesh axis runs over, the one named last changes fastest.
Arguments:
- states: bfloat16 [16, 8, 2048, 2048], P('member', None, 'tile'), may hold values from -8 to 8
- obs_var: float32 [8], replicated, may hold values from 2 to 30
- relax_rate: float32 [8], replicated, may hold values from 0.3 to 1
Outputs:
- nudged: bfloat16 [16, 8, 2048, 2048], P('member', None, 'tile')
- spread: float32 [8, 256, 256], P(None, 'tile')
All inputs are finite; a program needn't handle non-finite values.
Results may differ from a plain program's by a relative error of at most 0.0034.
Values may be sent and summed in bfloat16 or wider, within the bound.
No kernel may reach another device: no remote copies, remote signals or barrier semaphores. Data moves between devices by JAX's collectives and lax.ppermute only.
A program may use at most 64 MiB of HBM per device.

v0:
```python
import math
import jax
import jax.numpy as jnp
from jax import lax
from jax.sharding import PartitionSpec as P

NX = 2048
MODES = 256


def copy_for_each(shard, axis):
    copies = jnp.broadcast_to(shard, (lax.axis_size(axis), *shard.shape))
    return lax.all_to_all(copies, axis, split_axis=0, concat_axis=0, tiled=True)


def taken_together(shard, axis):
    everything = copy_for_each(shard, axis)
    return jnp.sum(everything, axis=0)


def in_one(arrays, axis):
    ends = [0]
    for a in arrays:
        ends.append(ends[-1] + a.size)
    running = taken_together(jnp.concatenate([a.ravel() for a in arrays]), axis)
    return tuple((running[b:e].reshape(a.shape) for a, b, e in zip(arrays, ends, ends[1:])))


def mode_table(positions, extent, mode_count):
    mode_index = jnp.arange(mode_count, dtype=jnp.int32)[None, :]
    wavenum = (mode_index + 1) // 2
    phases = positions[:, None] * wavenum % extent
    angles = 2.0 * math.pi / extent * phases.astype(jnp.float32)
    scaled = jnp.where(mode_index % 2 == 1, jnp.sin(angles), jnp.cos(angles))
    factor = jnp.where(mode_index == 0, math.sqrt(1.0 / extent), math.sqrt(2.0 / extent))
    return scaled * factor


def per_device(states, obs_var, relax_rate):
    layer_field = states[0]
    levels, row_count, col_count = layer_field.shape
    by_half = mode_table(jnp.arange(col_count, dtype=jnp.int32), col_count, MODES).astype(
        jnp.bfloat16
    )
    projected = jnp.dot(
        layer_field.reshape(levels * row_count, col_count),
        by_half,
        preferred_element_type=jnp.float32,
    )
    projected = projected.reshape(levels, row_count, MODES)
    table_full = mode_table(jnp.arange(NX, dtype=jnp.int32), NX, MODES)
    gathered_rows = lax.all_to_all(projected, "tile", split_axis=2, concat_axis=1, tiled=True)
    item_count, full_rows, block_cols = gathered_rows.shape
    flat_rows = jnp.transpose(gathered_rows, (1, 0, 2)).reshape(full_rows, item_count * block_cols)
    product = jnp.dot(
        table_full.T, flat_rows, precision=lax.Precision.HIGHEST, preferred_element_type=jnp.float32
    )
    product = jnp.transpose(product.reshape(MODES, item_count, block_cols), (1, 0, 2))
    coeffs = lax.all_to_all(product, "tile", split_axis=1, concat_axis=2, tiled=True)
    members = lax.axis_size("member")
    owner_mask = (lax.axis_index("member") == 0).astype(jnp.float32)
    totals, driver = in_one((coeffs, coeffs * owner_mask), "member")
    centered = coeffs - totals / members
    spread = taken_together(centered * centered, "member") / members
    departure = coeffs - driver
    weight_gain = relax_rate[:, None, None] * spread / (spread + obs_var[:, None, None])
    misfit = -weight_gain * departure
    misfit_cols = lax.all_to_all(misfit, "tile", split_axis=2, concat_axis=1, tiled=True)
    block_cols = misfit_cols.shape[2]
    flat_misfit = jnp.transpose(misfit_cols, (1, 0, 2)).reshape(MODES, levels * block_cols)
    wide_flat = jnp.dot(
        table_full, flat_misfit, precision=lax.Precision.HIGHEST, preferred_element_type=jnp.float32
    )
    wide_rows = jnp.transpose(wide_flat.reshape(NX, levels, block_cols), (1, 0, 2)).astype(
        jnp.bfloat16
    )
    rows_back = lax.all_to_all(wide_rows, "tile", split_axis=1, concat_axis=2, tiled=True)
    increment = jnp.dot(
        rows_back.reshape(levels * row_count, MODES), by_half.T, preferred_element_type=jnp.float32
    )
    increment = increment.reshape(levels, row_count, col_count)
    nudged = (layer_field.astype(jnp.float32) + increment).astype(jnp.bfloat16)
    return (nudged[None], spread)


def solution(mesh):
    in_specs = (P("member", None, "tile", None), P(), P())
    out_specs = (P("member", None, "tile", None), P(None, "tile", None))
    return jax.shard_map(
        per_device, mesh=mesh, in_specs=in_specs, out_specs=out_specs, check_vma=False
    )
```

profile of v0, /device:TPU:8, one launch (start us, length us, event | category | flops | bytes accessed | tf_op | source)
XLA Modules:
  0.0 251.9 jit_solution(14586560933564707945)
XLA Ops:
  0.7 11.3 %convolution_bitcast_fusion = f32[512,256]{0,1:T(8,128)S(1)} fusion(bf16[512,2048]{1,0:T(8,128)(2,1)} %bitcast.89, f32[256]{0:T(256)S(1)} %compare_select_fusion, s32[256]{0:T(256)S(1)} %and_select_fusion, pred[256]{0:T(512)(128)(4,1)S(1)} %fusion.22), kind=kOutput, calls=%fused_computation.18 | convolution fusion | flops 545783808 | bytes 2623744 | tf_op jit(solution)/shard_map/dot_general | solution.py:45
  12.0 0.2 copy.50
  12.2 0.4 copy.51
  12.6 0.7 reshape.125
  13.3 30.2 %all_to_all.80 = f32[32,1,4096]{2,1,0:T(1,128)S(1)} all-to-all(f32[32,1,4096]{2,1,0:T(1,128)S(1)} %reshape.125), channel_id=1, replica_groups=mesh['member'=16,'tile'=32] {'tile'}, dimensions={0} | all-to-all | bytes 1048576 | tf_op jit(solution)/shard_map/all_to_all | solution.py:52
  43.5 0.6 broadcast.153
  44.1 1.9 reduce.1
  46.0 0.4 reshape.126
  46.5 0.6 copy.53
  47.1 0.4 all_to_all.60
  47.4 9.9 %fusion.12 = f32[8,256,8]{1,2,0:T(8,128)S(1)} fusion(f32[256]{0:T(256)S(1)} %compare_select_fusion, s32[256]{0:T(256)S(1)} %and_select_fusion, pred[256]{0:T(512)(128)(4,1)S(1)} %fusion.22, f32[8,2048,8]{1,2,0:T(8,128)S(1)} %all_to_all.60), kind=kOutput, calls=%fused_computation.19 | convolution fusion | flops 411041792 | bytes 592128 | tf_op jit(solution)/shard_map/dot_general | solution.py:55
  57.4 0.4 copy.54
  57.8 1.2 reshape.127
  58.9 5.7 %all-to-all-start.1 = ((f32[32,1,512]{2,1,0:T(1,128)}), f32[32,1,512]{2,1,0:T(1,128)S(1)}, u32[]{:S(2)}, u32[]{:S(2)}) async-start(f32[32,1,512]{2,1,0:T(1,128)} %reshape.127), calls=%async_computation.1 | async-start | bytes 131072 | tf_op jit(solution)/shard_map/all_to_all | solution.py:59
  64.6 9.1 %all-to-all-done.1 = f32[32,1,512]{2,1,0:T(1,128)S(1)} async-done(((f32[32,1,512]{2,1,0:T(1,128)}), f32[32,1,512]{2,1,0:T(1,128)S(1)}, u32[]{:S(2)}, u32[]{:S(2)}) %all-to-all-start.1) | async-done | bytes 65568 | tf_op jit(solution)/shard_map/all_to_all | solution.py:59
  73.7 0.8 reduce.2
  74.6 0.6 reshape.128
  75.2 0.6 copy.56
  75.8 0.5 reshape.120
  76.3 2.9 %broadcast_in_dim.45 = f32[16,1,32768]{2,1,0:T(1,128)} broadcast(f32[32768]{0:T(1024)S(1)} %pad_maximum_fusion), dimensions={2} | broadcast | bytes 2228224 | tf_op jit(solution)/shard_map/broadcast_in_dim | solution.py:12
  79.2 7.0 %all-to-all-start.2 = ((f32[16,1,32768]{2,1,0:T(1,128)}), f32[16,1,32768]{2,1,0:T(1,128)S(1)}, u32[]{:S(2)}, u32[]{:S(2)}) async-start(f32[16,1,32768]{2,1,0:T(1,128)} %broadcast_in_dim.45), calls=%async_computation.2 | async-start | bytes 4194304 | tf_op jit(solution)/shard_map/all_to_all | solution.py:13
  86.2 0.5 all_to_all.64
  86.7 53.7 %all-to-all-done.2 = f32[16,1,32768]{2,1,0:T(1,128)S(1)} async-done(((f32[16,1,32768]{2,1,0:T(1,128)}), f32[16,1,32768]{2,1,0:T(1,128)S(1)}, u32[]{:S(2)}, u32[]{:S(2)}) %all-to-all-start.2) | async-done | bytes 2097184 | tf_op jit(solution)/shard_map/all_to_all | solution.py:13
  140.4 1.4 reduce_sum.18
  141.8 0.0 copy-start.2
  141.9 0.0 copy-start
  141.9 1.1 broadcast_in_dim.46
  143.0 3.7 %all-to-all-start.3 = ((f32[16,8,8,256]{3,2,1,0:T(8,128)}), f32[16,8,8,256]{3,2,1,0:T(8,128)S(1)}, u32[]{:S(2)}, u32[]{:S(2)}) async-start(f32[16,8,8,256]{3,2,1,0:T(8,128)} %broadcast_in_dim.46), calls=%async_computation.3 | async-start | bytes 2097152 | tf_op jit(solution)/shard_map/all_to_all | solution.py:13
  146.6 0.0 copy-done.2
  146.7 20.3 %all-to-all-done.3 = f32[16,8,8,256]{3,2,1,0:T(8,128)S(1)} async-done(((f32[16,8,8,256]{3,2,1,0:T(8,128)}), f32[16,8,8,256]{3,2,1,0:T(8,128)S(1)}, u32[]{:S(2)}, u32[]{:S(2)}) %all-to-all-start.3) | async-done | bytes 1048608 | tf_op jit(solution)/shard_map/all_to_all | solution.py:13
  167.0 0.1 reduce_sum.19
  167.1 0.0 copy-done
  167.1 0.6 subtract_multiply_fusion
  167.7 0.4 copy.59
  168.1 0.5 reshape.129
  168.7 23.7 %all_to_all.81 = f32[32,1,512]{2,1,0:T(1,128)S(1)} all-to-all(f32[32,1,512]{2,1,0:T(1,128)S(1)} %reshape.129), channel_id=1, replica_groups=mesh['member'=16,'tile'=32] {'tile'}, dimensions={0} | all-to-all | bytes 131072 | tf_op jit(solution)/shard_map/all_to_all | solution.py:68
  192.4 0.8 reduce.3
  193.2 0.6 reshape.130
  193.8 0.6 copy.61
  194.4 0.5 all_to_all.70
  195.0 11.4 %fusion.2 = bf16[8,2048,8]{1,2,0:T(8,128)(2,1)S(1)} fusion(f32[256]{0:T(256)S(1)} %compare_select_fusion, s32[256]{0:T(256)S(1)} %and_select_fusion, pred[256]{0:T(512)(128)(4,1)S(1)} %fusion.22, f32[8,256,8]{1,2,0:T(8,128)S(1)} %all_to_all.70), kind=kOutput, calls=%fused_computation.7 | convolution fusion | flops 411172864 | bytes 329984 | tf_op jit(solution)/shard_map/dot_general | solution.py:71
  206.4 4.0 %copy.62 = bf16[8,2048,8]{2,0,1:T(8,128)(2,1)} copy(bf16[8,2048,8]{1,2,0:T(8,128)(2,1)S(1)} %fusion.2) | data formatting | bytes 524288 | tf_op jit(solution)/shard_map/convert_element_type | solution.py:74
  210.4 5.8 %reshape.131 = bf16[32,2,2048]{2,1,0:T(2,128)(2,1)S(1)} reshape(bf16[2048,8,8]{2,1,0:T(8,128)(2,1)} %bitcast.80) | data formatting | bytes 524288
  216.2 14.0 %all_to_all.82 = bf16[32,2,2048]{2,1,0:T(2,128)(2,1)S(1)} all-to-all(bf16[32,2,2048]{2,1,0:T(2,128)(2,1)S(1)} %reshape.131), channel_id=1, replica_groups=mesh['member'=16,'tile'=32] {'tile'}, dimensions={0} | all-to-all | bytes 524288 | tf_op jit(solution)/shard_map/all_to_all | solution.py:77
  230.2 5.9 %reshape.132 = bf16[2048,8,8]{2,1,0:T(8,128)(2,1)} reshape(bf16[32,2,2048]{2,1,0:T(2,128)(2,1)S(1)} %all_to_all.82) | data formatting | bytes 524288
  236.2 0.0 copy-start.1
  236.2 4.6 %copy.63 = bf16[8,32,64,8]{2,3,1,0:T(8,128)(2,1)S(1)} copy(bf16[8,32,64,8]{3,0,2,1:T(8,128)(2,1)} %bitcast.81) | data formatting | bytes 524288 | tf_op jit(solution)/shard_map/all_to_all | solution.py:77
  240.8 0.0 copy-done.1
  240.8 11.1 %fusion.1 = bf16[1,8,64,2048]{3,2,1,0:T(8,128)(2,1)} fusion(bf16[1,8,64,2048]{3,2,1,0:T(8,128)(2,1)S(1)} %copy-done.1, f32[256]{0:T(256)S(1)} %compare_select_fusion, s32[256]{0:T(256)S(1)} %and_select_fusion, pred[256]{0:T(512)(128)(4,1)S(1)} %fusion.22, bf16[8,32,64,8]{2,3,1,0:T(8,128)(2,1)S(1)} %copy.63), kind=kOutput, calls=%fused_computation.5 | convolution fusion | flops 548929536 | bytes 4458752 | tf_op jit(solution)/shard_map/dot_general | solution.py:78
  (10 shorter events, 0.1 us)
Async XLA Ops:
  58.9 14.8 %all-to-all-start.1 = ((f32[32,1,512]{2,1,0:T(1,128)}), f32[32,1,512]{2,1,0:T(1,128)S(1)}, u32[]{:S(2)}, u32[]{:S(2)}) async-start(f32[32,1,512]{2,1,0:T(1,128)} %reshape.127), calls=%async_computation.1 | async-start | bytes 131072 | tf_op jit(solution)/shard_map/all_to_all | solution.py:59
  79.2 61.2 %all-to-all-start.2 = ((f32[16,1,32768]{2,1,0:T(1,128)}), f32[16,1,32768]{2,1,0:T(1,128)S(1)}, u32[]{:S(2)}, u32[]{:S(2)}) async-start(f32[16,1,32768]{2,1,0:T(1,128)} %broadcast_in_dim.45), calls=%async_computation.2 | async-start | bytes 4194304 | tf_op jit(solution)/shard_map/all_to_all | solution.py:13
  141.8 4.8 %copy-start.2 = (f32[8]{0:T(128)S(1)}, f32[8]{0:T(128)}, u32[]{:S(2)}) copy-start(f32[8]{0:T(128)} %param.5) | copy-start | bytes 100
  141.9 25.2 %copy-start = (f32[8]{0:T(128)S(1)}, f32[8]{0:T(128)}, u32[]{:S(2)}) copy-start(f32[8]{0:T(128)} %param.4) | copy-start | bytes 100
  143.0 24.0 %all-to-all-start.3 = ((f32[16,8,8,256]{3,2,1,0:T(8,128)}), f32[16,8,8,256]{3,2,1,0:T(8,128)S(1)}, u32[]{:S(2)}, u32[]{:S(2)}) async-start(f32[16,8,8,256]{3,2,1,0:T(8,128)} %broadcast_in_dim.46), calls=%async_computation.3 | async-start | bytes 2097152 | tf_op jit(solution)/shard_map/all_to_all | solution.py:13
  236.2 4.6 %copy-start.1 = (bf16[1,8,64,2048]{3,2,1,0:T(8,128)(2,1)S(1)}, bf16[1,8,64,2048]{3,2,1,0:T(8,128)(2,1)}, u32[]{:S(2)}) copy-start(bf16[1,8,64,2048]{3,2,1,0:T(8,128)(2,1)} %param.3) | copy-start | bytes 6291460
where the time goes:
time: 252 us
  waiting for transfers between devices  83.1 us (33%)
  blocking collectives  68 us (27%)
  matrix products  43.7 us (17%)
  local copies, waits for them, and re-layouts  34.1 us (14%)
  starting transfers between devices  16.3 us (6%)
  other arithmetic  5.76 us (2%)
    all_to_all x2, waiting for transfers between devices, copy_for_each(): return lax.all_to_all(copies, axis, split_axis=0, concat_axis=0, tiled=True)  74 us
    all_to_all x1, blocking collectives, per_device(): lax.all_to_all(projected, 'tile', split_axis=2, concat_axis=1, tiled=True)  30.2 us
    all_to_all x1, blocking collectives, per_device(): lax.all_to_all(misfit, 'tile', split_axis=2, concat_axis=1, tiled=True)  23.7 us
    unnamed x14, local copies, waits for them, and re-layouts  15.6 us
    all_to_all x1, blocking collectives, per_device(): lax.all_to_all(wide_rows, 'tile', split_axis=1, concat_axis=2, tiled=True)  14 us
    dot_general x1, matrix products, per_device(): jnp.dot(table_full, flat_misfit, precision=lax.Precision.HIGHEST, preferr...  11.4 us
    dot_general x1, matrix products, per_device(): jnp.dot(layer_field.reshape(levels * row_count, col_count), by_half, pref...  11.3 us
    dot_general x1, matrix products, per_device(): jnp.dot(rows_back.reshape(levels * row_count, MODES), by_half.T, preferre...  11.1 us
  transfers between devices with their start and end apart: 3, of which 3 were waited for; matrix products, arithmetic and copies ran while one was open for 0% of the time, Pallas kernels for 0%

commit v1 on v0

--- a/solution.py
+++ b/solution.py
@@ -74,7 +74,12 @@
     wide_rows = jnp.transpose(wide_flat.reshape(NX, levels, block_cols), (1, 0, 2)).astype(
         jnp.bfloat16
     )
-    rows_back = lax.all_to_all(wide_rows, "tile", split_axis=1, concat_axis=2, tiled=True)
+    rows_back = jnp.concatenate(
+        lax.all_to_all(
+            jnp.stack(jnp.split(wide_rows, lax.axis_size("tile"), axis=1)), "tile", 0, 0
+        ),
+        axis=2,
+    )
     increment = jnp.dot(
         rows_back.reshape(levels * row_count, MODES), by_half.T, preferred_element_type=jnp.float32
     )

time: 252 us -> 234 us (0.929)
  local copies, waits for them, and re-layouts: 34.1 us -> 16.1 us
    unnamed x14 -> x45, local copies, waits for them, and re-layouts: 15.6 us -> 6.16 us
    all_to_all x1 -> x0, local copies, waits for them, and re-layouts: 4.64 us -> none  [per_device(): lax.all_to_all(wide_rows, 'tile', split_axis=1, concat_axis=2, tiled=True)]
    convert_element_type x1 -> x0, local copies, waits for them, and re-layouts: 4.02 us -> none  [per_device(): jnp.transpose(wide_flat.reshape(NX, levels, block_cols), (1, 0, 2))]
where the time goes in v1:
time: 234 us; the launch traced here: 233 us
  waiting for transfers between devices  83.1 us (36%)
  blocking collectives  68 us (29%)
  matrix products  43.1 us (18%)
  starting transfers between devices  16.3 us (7%)
  local copies, waits for them, and re-layouts  16.1 us (7%)
  other arithmetic  5.76 us (2%)
    all_to_all x2, waiting for transfers between devices, copy_for_each(): return lax.all_to_all(copies, axis, split_axis=0, concat_axis=0, tiled=True)  74 us
    all_to_all x1, blocking collectives, per_device(): lax.all_to_all(projected, 'tile', split_axis=2, concat_axis=1, tiled=True)  30.2 us
    all_to_all x1, blocking collectives, per_device(): lax.all_to_all(misfit, 'tile', split_axis=2, concat_axis=1, tiled=True)  23.7 us
    all_to_all x1, blocking collectives, per_device(): lax.all_to_all(jnp.stack(jnp.split(wide_rows, lax.axis_size('tile'), axis...  14 us
    dot_general x1, matrix products, per_device(): jnp.dot(table_full, flat_misfit, precision=lax.Precision.HIGHEST, preferr...  11.4 us
    dot_general x1, matrix products, per_device(): jnp.dot(layer_field.reshape(levels * row_count, col_count), by_half, pref...  11.3 us
    all_to_all x2, starting transfers between devices, copy_for_each(): return lax.all_to_all(copies, axis, split_axis=0, concat_axis=0, tiled=True)  10.6 us
    dot_general x1, matrix products, per_device(): jnp.dot(rows_back.reshape(levels * row_count, MODES), by_half.T, preferre...  10.4 us
  transfers between devices with their start and end apart: 3, of which 3 were waited for; matrix products, arithmetic and copies ran while one was open for 0% of the time, Pallas kernels for 0%

profile of v1, /device:TPU:8, one launch (start us, length us, event | category | flops | bytes accessed | tf_op | source)
XLA Modules:
  0.0 233.3 jit_solution(17899990971272884790)
XLA Ops:
  0.7 11.3 %convolution_bitcast_fusion = f32[512,256]{0,1:T(8,128)S(1)} fusion(bf16[512,2048]{1,0:T(8,128)(2,1)} %bitcast.220, f32[256]{0:T(256)S(1)} %compare_select_fusion, s32[256]{0:T(256)S(1)} %and_select_fusion, pred[256]{0:T(512)(128)(4,1)S(1)} %fusion.23), kind=kOutput, calls=%fused_computation.18 | convolution fusion | flops 545783808 | bytes 2623744 | tf_op jit(solution)/shard_map/dot_general | solution.py:45
  12.0 0.2 copy.47
  12.2 0.4 copy.48
  12.6 0.7 reshape.127
  13.3 30.2 %all_to_all.70 = f32[32,1,4096]{2,1,0:T(1,128)S(1)} all-to-all(f32[32,1,4096]{2,1,0:T(1,128)S(1)} %reshape.127), channel_id=1, replica_groups=mesh['member'=16,'tile'=32] {'tile'}, dimensions={0} | all-to-all | bytes 1048576 | tf_op jit(solution)/shard_map/all_to_all | solution.py:52
  43.5 0.6 broadcast.153
  44.1 1.9 reduce.1
  46.0 0.4 reshape.128
  46.5 0.6 copy.50
  47.1 0.4 all_to_all.52
  47.4 9.9 %fusion.12 = f32[8,256,8]{1,2,0:T(8,128)S(1)} fusion(f32[256]{0:T(256)S(1)} %compare_select_fusion, s32[256]{0:T(256)S(1)} %and_select_fusion, pred[256]{0:T(512)(128)(4,1)S(1)} %fusion.23, f32[8,2048,8]{1,2,0:T(8,128)S(1)} %all_to_all.52), kind=kOutput, calls=%fused_computation.19 | convolution fusion | flops 411041792 | bytes 592128 | tf_op jit(solution)/shard_map/dot_general | solution.py:55
  57.4 0.4 copy.51
  57.8 1.2 reshape.129
  58.9 5.7 %all-to-all-start.1 = ((f32[32,1,512]{2,1,0:T(1,128)}), f32[32,1,512]{2,1,0:T(1,128)S(1)}, u32[]{:S(2)}, u32[]{:S(2)}) async-start(f32[32,1,512]{2,1,0:T(1,128)} %reshape.129), calls=%async_computation.1 | async-start | bytes 131072 | tf_op jit(solution)/shard_map/all_to_all | solution.py:59
  64.6 9.1 %all-to-all-done.1 = f32[32,1,512]{2,1,0:T(1,128)S(1)} async-done(((f32[32,1,512]{2,1,0:T(1,128)}), f32[32,1,512]{2,1,0:T(1,128)S(1)}, u32[]{:S(2)}, u32[]{:S(2)}) %all-to-all-start.1) | async-done | bytes 65568 | tf_op jit(solution)/shard_map/all_to_all | solution.py:59
  73.7 0.8 reduce.2
  74.6 0.6 reshape.130
  75.2 0.6 copy.53
  75.8 0.5 reshape.121
  76.3 2.9 %broadcast_in_dim.45 = f32[16,1,32768]{2,1,0:T(1,128)} broadcast(f32[32768]{0:T(1024)S(1)} %pad_maximum_fusion), dimensions={2} | broadcast | bytes 2228224 | tf_op jit(solution)/shard_map/broadcast_in_dim | solution.py:12
  79.2 7.0 %all-to-all-start.2 = ((f32[16,1,32768]{2,1,0:T(1,128)}), f32[16,1,32768]{2,1,0:T(1,128)S(1)}, u32[]{:S(2)}, u32[]{:S(2)}) async-start(f32[16,1,32768]{2,1,0:T(1,128)} %broadcast_in_dim.45), calls=%async_computation.2 | async-start | bytes 4194304 | tf_op jit(solution)/shard_map/all_to_all | solution.py:13
  86.2 0.5 all_to_all.56
  86.7 53.7 %all-to-all-done.2 = f32[16,1,32768]{2,1,0:T(1,128)S(1)} async-done(((f32[16,1,32768]{2,1,0:T(1,128)}), f32[16,1,32768]{2,1,0:T(1,128)S(1)}, u32[]{:S(2)}, u32[]{:S(2)}) %all-to-all-start.2) | async-done | bytes 2097184 | tf_op jit(solution)/shard_map/all_to_all | solution.py:13
  140.4 1.4 reduce_sum.18
  141.8 0.0 copy-start.2
  141.9 0.0 copy-start
  141.9 1.1 broadcast_in_dim.46
  143.0 3.7 %all-to-all-start.3 = ((f32[16,8,8,256]{3,2,1,0:T(8,128)}), f32[16,8,8,256]{3,2,1,0:T(8,128)S(1)}, u32[]{:S(2)}, u32[]{:S(2)}) async-start(f32[16,8,8,256]{3,2,1,0:T(8,128)} %broadcast_in_dim.46), calls=%async_computation.3 | async-start | bytes 2097152 | tf_op jit(solution)/shard_map/all_to_all | solution.py:13
  146.6 0.0 copy-done.2
  146.7 20.3 %all-to-all-done.3 = f32[16,8,8,256]{3,2,1,0:T(8,128)S(1)} async-done(((f32[16,8,8,256]{3,2,1,0:T(8,128)}), f32[16,8,8,256]{3,2,1,0:T(8,128)S(1)}, u32[]{:S(2)}, u32[]{:S(2)}) %all-to-all-start.3) | async-done | bytes 1048608 | tf_op jit(solution)/shard_map/all_to_all | solution.py:13
  167.0 0.1 reduce_sum.19
  167.1 0.0 copy-done
  167.1 0.6 subtract_multiply_fusion
  167.7 0.4 copy.56
  168.1 0.5 reshape.131
  168.7 23.7 %all_to_all.71 = f32[32,1,512]{2,1,0:T(1,128)S(1)} all-to-all(f32[32,1,512]{2,1,0:T(1,128)S(1)} %reshape.131), channel_id=1, replica_groups=mesh['member'=16,'tile'=32] {'tile'}, dimensions={0} | all-to-all | bytes 131072 | tf_op jit(solution)/shard_map/all_to_all | solution.py:68
  192.4 0.8 reduce.3
  193.2 0.6 reshape.132
  193.8 0.6 copy.58
  194.4 0.5 all_to_all.62
  195.0 11.4 %fusion.2 = bf16[8,2048,8]{1,2,0:T(8,128)(2,1)S(1)} fusion(f32[256]{0:T(256)S(1)} %compare_select_fusion, s32[256]{0:T(256)S(1)} %and_select_fusion, pred[256]{0:T(512)(128)(4,1)S(1)} %fusion.23, f32[8,256,8]{1,2,0:T(8,128)S(1)} %all_to_all.62), kind=kOutput, calls=%fused_computation.7 | convolution fusion | flops 411172864 | bytes 329984 | tf_op jit(solution)/shard_map/dot_general | solution.py:71
  206.4 0.0 copy-start.1
  206.4 0.1 constant_dynamic-update-slice_fusion.30
  206.6 0.1 constant_dynamic-update-slice_fusion.28
  206.7 0.1 constant_dynamic-update-slice_fusion.26
  206.8 0.1 constant_dynamic-update-slice_fusion.24
  206.9 0.1 constant_dynamic-update-slice_fusion.22
  207.0 0.1 constant_dynamic-update-slice_fusion.20
  207.1 0.1 constant_dynamic-update-slice_fusion.18
  207.2 0.1 constant_dynamic-update-slice_fusion.16
  207.3 0.1 constant_dynamic-update-slice_fusion.14
  207.4 0.1 constant_dynamic-update-slice_fusion.12
  207.5 0.1 constant_dynamic-update-slice_fusion.10
  207.6 0.1 constant_dynamic-update-slice_fusion.8
  207.7 0.1 constant_dynamic-update-slice_fusion.6
  207.8 0.1 constant_dynamic-update-slice_fusion.4
  207.9 0.1 constant_dynamic-update-slice_fusion.2
  208.0 0.1 constant_dynamic-update-slice_fusion
  208.1 0.4 reshape.133
  208.5 14.0 %all_to_all.72 = bf16[32,2,2048]{2,1,0:T(2,128)(2,1)S(1)} all-to-all(bf16[32,2,2048]{2,1,0:T(2,128)(2,1)S(1)} %reshape.133), channel_id=1, replica_groups=mesh['member'=16,'tile'=32] {'tile'}, dimensions={0} | all-to-all | bytes 524288 | tf_op jit(solution)/shard_map/all_to_all | solution.py:78
  222.5 0.4 reshape.134
  222.9 0.0 copy-done.1
  222.9 10.4 %fusion.1 = bf16[1,8,64,2048]{3,2,1,0:T(8,128)(2,1)} fusion(bf16[1,8,64,2048]{3,2,1,0:T(8,128)(2,1)S(1)} %copy-done.1, f32[256]{0:T(256)S(1)} %compare_select_fusion, s32[256]{0:T(256)S(1)} %and_select_fusion, pred[256]{0:T(512)(128)(4,1)S(1)} %fusion.23, bf16[32,8,8,64]{3,2,1,0:T(8,128)(2,1)S(1)} %reshape.134), kind=kOutput, calls=%fused_computation.5 | convolution fusion | flops 548929536 | bytes 4458752 | tf_op jit(solution)/shard_map/dot_general | solution.py:83
  (26 shorter events, 0.3 us)
Async XLA Ops:
  58.9 14.8 %all-to-all-start.1 = ((f32[32,1,512]{2,1,0:T(1,128)}), f32[32,1,512]{2,1,0:T(1,128)S(1)}, u32[]{:S(2)}, u32[]{:S(2)}) async-start(f32[32,1,512]{2,1,0:T(1,128)} %reshape.129), calls=%async_computation.1 | async-start | bytes 131072 | tf_op jit(solution)/shard_map/all_to_all | solution.py:59
  79.2 61.2 %all-to-all-start.2 = ((f32[16,1,32768]{2,1,0:T(1,128)}), f32[16,1,32768]{2,1,0:T(1,128)S(1)}, u32[]{:S(2)}, u32[]{:S(2)}) async-start(f32[16,1,32768]{2,1,0:T(1,128)} %broadcast_in_dim.45), calls=%async_computation.2 | async-start | bytes 4194304 | tf_op jit(solution)/shard_map/all_to_all | solution.py:13
  141.8 4.8 %copy-start.2 = (f32[8]{0:T(128)S(1)}, f32[8]{0:T(128)}, u32[]{:S(2)}) copy-start(f32[8]{0:T(128)} %param.5) | copy-start | bytes 100
  141.9 25.2 %copy-start = (f32[8]{0:T(128)S(1)}, f32[8]{0:T(128)}, u32[]{:S(2)}) copy-start(f32[8]{0:T(128)} %param.4) | copy-start | bytes 100
  143.0 24.0 %all-to-all-start.3 = ((f32[16,8,8,256]{3,2,1,0:T(8,128)}), f32[16,8,8,256]{3,2,1,0:T(8,128)S(1)}, u32[]{:S(2)}, u32[]{:S(2)}) async-start(f32[16,8,8,256]{3,2,1,0:T(8,128)} %broadcast_in_dim.46), calls=%async_computation.3 | async-start | bytes 2097152 | tf_op jit(solution)/shard_map/all_to_all | solution.py:13
  206.4 16.5 %copy-start.1 = (bf16[1,8,64,2048]{3,2,1,0:T(8,128)(2,1)S(1)}, bf16[1,8,64,2048]{3,2,1,0:T(8,128)(2,1)}, u32[]{:S(2)}) copy-start(bf16[1,8,64,2048]{3,2,1,0:T(8,128)(2,1)} %param.3) | copy-start | bytes 6291460
